TPU v7x, 32 devices: a whole 2x2x4 slice. The times are simulated.
32 devices in a mesh: seq: 4 (over y, core), head: 8 (over z, x).
Axes of the slice: x: 2, y: 2, z: 4, core: 2. Of those that a mesh axis runs over, the one named last changes fastest.
Arguments:
- query: bfloat16 [4096, 4096], P(('seq', 'head')), may hold values from -6 to 6
- key_matrix: bfloat16 [4096, 2048], P(('seq', 'head')), may hold values from -6 to 6
- value_matrix: bfloat16 [4096, 2048], P(('seq', 'head')), may hold values from -6 to 6
- output_gradient: bfloat16 [4096, 4096], P(('seq', 'head')), may hold values from -6 to 6
- attn_out: bfloat16 [4096, 4096], P(('seq', 'head')), may hold values from -3 to 3
- doc_offsets: int32 [9], replicated, may hold values from 0 to 4096, as said below
- stats: float32 [4096, 32], P(('seq', 'head')), may hold values from -1 to 9
Outputs:
- grad_query: bfloat16 [4096, 4096], P(('seq', 'head'))
- key_gradient: bfloat16 [4096, 2048], P(('seq', 'head'))
- value_gradient: bfloat16 [4096, 2048], P(('seq', 'head'))
Inputs may be any that keep to these rules, and one draw needn't show every extreme that they name: doc_offsets[0] is 0, doc_offsets[8] is 4096, the entries rise strictly; no document has more than 1023 tokens and one has exactly that many.
All inputs are finite; a program needn't handle non-finite values.
Results may differ from a plain program's by a relative error of at most 0.0063.
Values may be sent and summed in bfloat16 or wider, within the bound.
A program may use at most 64 MiB of HBM per device.

v0:
```python
import jax
import jax.numpy as jnp
from jax import lax
from jax.sharding import PartitionSpec as P

HQ = 32
HEAD_SIZE = 128
DOCHALF = 512
QBLK = 512
attn_scale = 144.0 ** (-0.5)


def partner(value, axis, apart):
    mask = 2**apart
    pairs = [(source, source ^ mask) for source in range(lax.axis_size(axis))]
    return lax.ppermute(value, axis, pairs)


def from_behind(value, axis, steps):
    count = lax.axis_size(axis)
    leading, last = (max(0, -steps), min(count, count - steps))
    return lax.ppermute(value, axis, [(source, source + steps) for source in range(leading, last)])


def tile_grads(query_rows, grad_rows, lse_rows, delta_rows, key_window, value_window, allowed):
    score = (
        jnp.einsum("qgrd,kgd->grqk", query_rows, key_window, preferred_element_type=jnp.float32)
        * attn_scale
    )
    norm_stat = jnp.transpose(lse_rows, (1, 2, 0))[..., None]
    prob = jnp.where(allowed[None, None], jnp.exp(score - norm_stat), 0.0)
    dprob = jnp.einsum(
        "qgrd,kgd->grqk", grad_rows, value_window, preferred_element_type=jnp.float32
    )
    dscore = prob * (dprob - jnp.transpose(delta_rows, (1, 2, 0))[..., None])
    prob_low = prob.astype(jnp.bfloat16)
    dscore_low = dscore.astype(jnp.bfloat16)
    value_gradient = jnp.einsum(
        "grqk,qgrd->kgd", prob_low, grad_rows, preferred_element_type=jnp.float32
    )
    key_gradient = (
        jnp.einsum("grqk,qgrd->kgd", dscore_low, query_rows, preferred_element_type=jnp.float32)
        * attn_scale
    )
    grad_query = (
        jnp.einsum("grqk,kgd->qgrd", dscore_low, key_window, preferred_element_type=jnp.float32)
        * attn_scale
    )
    return (grad_query, key_gradient, value_gradient)


def doc_numbers(positions, inner):
    return jnp.sum((inner[None, :] <= positions[:, None]).astype(jnp.int32), axis=1)


def shards(query, key_matrix, value_matrix, output_gradient, attn_out, doc_offsets, stats):
    token_count_local = query.shape[0]
    members = lax.axis_size("head")
    group_span = token_count_local * members
    per_device = HQ // members
    lookback = 2 * DOCHALF
    width = lookback + QBLK
    group = lax.axis_index("seq")
    member = lax.axis_index("head")
    parity = member % 2
    half_width = HEAD_SIZE // 2
    delta_correction = jnp.sum(
        (output_gradient.astype(jnp.float32) * attn_out.astype(jnp.float32)).reshape(
            token_count_local, HQ, HEAD_SIZE
        ),
        axis=2,
    )
    query_heads, grad_heads = (
        lax.all_to_all(query, "head", split_axis=1, concat_axis=0, tiled=True),
        lax.all_to_all(output_gradient, "head", split_axis=1, concat_axis=0, tiled=True),
    )
    lse_heads, delta_heads = (
        lax.all_to_all(stats, "head", split_axis=1, concat_axis=0, tiled=True),
        lax.all_to_all(delta_correction, "head", split_axis=1, concat_axis=0, tiled=True),
    )
    key_cols, value_cols = (
        lax.all_to_all(key_matrix, "head", split_axis=1, concat_axis=0, tiled=True),
        lax.all_to_all(value_matrix, "head", split_axis=1, concat_axis=0, tiled=True),
    )
    if per_device >= 2:
        groups = per_device // 2
        key_heads = key_cols.reshape(group_span, groups, HEAD_SIZE)
        value_heads = value_cols.reshape(group_span, groups, HEAD_SIZE)
    else:
        groups = 1
        other_key, other_value = partner((key_cols, value_cols), "head", 0)
        key_heads = jnp.where(
            parity == 0,
            jnp.concatenate([key_cols, other_key], 1),
            jnp.concatenate([other_key, key_cols], 1),
        ).reshape(group_span, 1, HEAD_SIZE)
        value_heads = jnp.where(
            parity == 0,
            jnp.concatenate([value_cols, other_value], 1),
            jnp.concatenate([other_value, value_cols], 1),
        ).reshape(group_span, 1, HEAD_SIZE)
    repeats = per_device // groups
    query_heads = query_heads.reshape(group_span, groups, repeats, HEAD_SIZE)
    grad_heads = grad_heads.reshape(group_span, groups, repeats, HEAD_SIZE)
    lse_heads = lse_heads.reshape(group_span, groups, repeats)
    delta_heads = delta_heads.reshape(group_span, groups, repeats)
    prior_key, prior_value = from_behind(
        (key_heads[group_span - lookback :], value_heads[group_span - lookback :]), "seq", 1
    )
    key_ext = jnp.concatenate([prior_key, key_heads], 0)
    value_ext = jnp.concatenate([prior_value, value_heads], 0)
    inner = doc_offsets[1:-1]
    query_pos = group * group_span + jnp.arange(group_span, dtype=jnp.int32)
    key_pos = group * group_span - lookback + jnp.arange(lookback + group_span, dtype=jnp.int32)
    query_doc = doc_numbers(query_pos, inner)
    key_doc = doc_numbers(key_pos, inner)

    def block_step(block, carry):
        grad_q, grad_k, grad_v = carry
        start = (block * QBLK).astype(jnp.int32)
        query_rows = lax.dynamic_slice_in_dim(query_heads, start, QBLK, 0)
        grad_rows = lax.dynamic_slice_in_dim(grad_heads, start, QBLK, 0)
        lse_rows = lax.dynamic_slice_in_dim(lse_heads, start, QBLK, 0)
        delta_rows = lax.dynamic_slice_in_dim(delta_heads, start, QBLK, 0)
        key_window = lax.dynamic_slice_in_dim(key_ext, start, width, 0)
        value_window = lax.dynamic_slice_in_dim(value_ext, start, width, 0)
        rows_pos = lax.dynamic_slice_in_dim(query_pos, start, QBLK, 0)
        rows_doc = lax.dynamic_slice_in_dim(query_doc, start, QBLK, 0)
        cols_pos = lax.dynamic_slice_in_dim(key_pos, start, width, 0)
        cols_doc = lax.dynamic_slice_in_dim(key_doc, start, width, 0)
        allowed = (
            (cols_doc[None, :] == rows_doc[:, None])
            & (cols_pos[None, :] <= rows_pos[:, None])
            & (cols_pos[None, :] >= 0)
        )
        block_q, block_k, block_v = tile_grads(
            query_rows, grad_rows, lse_rows, delta_rows, key_window, value_window, allowed
        )
        grad_q = lax.dynamic_update_slice_in_dim(grad_q, block_q, start, 0)
        grad_k = lax.dynamic_update_slice_in_dim(
            grad_k, lax.dynamic_slice_in_dim(grad_k, start, width, 0) + block_k, start, 0
        )
        grad_v = lax.dynamic_update_slice_in_dim(
            grad_v, lax.dynamic_slice_in_dim(grad_v, start, width, 0) + block_v, start, 0
        )
        return (grad_q, grad_k, grad_v)

    init = (
        jnp.zeros((group_span, groups, repeats, HEAD_SIZE), jnp.float32),
        jnp.zeros((lookback + group_span, groups, HEAD_SIZE), jnp.float32),
        jnp.zeros((lookback + group_span, groups, HEAD_SIZE), jnp.float32),
    )
    grad_q, grad_k, grad_v = lax.fori_loop(0, group_span // QBLK, block_step, init)
    back_key, back_value = (
        from_behind(grad_k[:lookback].astype(jnp.bfloat16), "seq", -1).astype(jnp.float32),
        from_behind(grad_v[:lookback].astype(jnp.bfloat16), "seq", -1).astype(jnp.float32),
    )
    own_key = grad_k[lookback:].at[group_span - lookback :].add(back_key)
    own_value = grad_v[lookback:].at[group_span - lookback :].add(back_value)
    query_low = grad_q.astype(jnp.bfloat16).reshape(group_span, per_device * HEAD_SIZE)
    grad_query = lax.all_to_all(query_low, "head", split_axis=0, concat_axis=1, tiled=True)
    if per_device >= 2:
        send_key = own_key.reshape(group_span, groups * HEAD_SIZE)
        send_value = own_value.reshape(group_span, groups * HEAD_SIZE)
    else:
        flat_key = own_key.reshape(group_span, HEAD_SIZE)
        flat_value = own_value.reshape(group_span, HEAD_SIZE)
        keep_key = lax.dynamic_slice_in_dim(flat_key, parity * half_width, half_width, 1)
        keep_value = lax.dynamic_slice_in_dim(flat_value, parity * half_width, half_width, 1)
        give_key = lax.dynamic_slice_in_dim(flat_key, (1 - parity) * half_width, half_width, 1)
        give_value = lax.dynamic_slice_in_dim(flat_value, (1 - parity) * half_width, half_width, 1)
        from_key, from_value = partner((give_key, give_value), "head", 0)
        send_key = keep_key + from_key
        send_value = keep_value + from_value
    key_gradient_summed, value_gradient_summed = (
        lax.all_to_all(
            send_key.astype(jnp.bfloat16), "head", split_axis=0, concat_axis=1, tiled=True
        ).astype(send_key.dtype),
        lax.all_to_all(
            send_value.astype(jnp.bfloat16), "head", split_axis=0, concat_axis=1, tiled=True
        ).astype(send_value.dtype),
    )
    key_gradient = key_gradient_summed.astype(jnp.bfloat16)
    value_gradient = value_gradient_summed.astype(jnp.bfloat16)
    return (grad_query, key_gradient, value_gradient)


def solution(mesh):
    placed = (
        P(("seq", "head"), None),
        P(("seq", "head"), None),
        P(("seq", "head"), None),
        P(("seq", "head"), None),
        P(("seq", "head"), None),
        P(),
        P(("seq", "head"), None),
    )
    return jax.shard_map(
        shards,
        mesh=mesh,
        in_specs=placed,
        out_specs=(P(("seq", "head"), None), P(("seq", "head"), None), P(("seq", "head"), None)),
        check_vma=False,
    )
```

profile of v0, /device:TPU:1, one launch (start us, length us, event | category | flops | bytes accessed | tf_op | source)
XLA Modules:
  0.0 241.6 jit_solution(3520835461747851998)
XLA Ops:
  0.6 6.4 %all-to-all-start.2 = ((f32[128,8,4]{0,2,1:T(4,128)}), f32[128,8,4]{0,2,1:T(4,128)S(1)}, u32[]{:S(2)}, u32[]{:S(2)}) async-start(f32[128,8,4]{0,2,1:T(4,128)} %bitcast.171), calls=%async_computation.2 | async-start | bytes 32768 | tf_op jit(solution)/shard_map/all_to_all | solution.py:78
  12.4 3.5 %all-to-all-start.5 = ((f32[128,8,4]{0,2,1:T(4,128)}), f32[128,8,4]{0,2,1:T(4,128)S(1)}, u32[]{:S(2)}, u32[]{:S(2)}) async-start(f32[128,8,4]{0,2,1:T(4,128)} %bitcast.26), calls=%async_computation.5 | async-start | bytes 32768 | tf_op jit(solution)/shard_map/all_to_all | solution.py:79
  18.0 3.4 %all-to-all-done.5 = f32[128,8,4]{0,2,1:T(4,128)S(1)} async-done(((f32[128,8,4]{0,2,1:T(4,128)}), f32[128,8,4]{0,2,1:T(4,128)S(1)}, u32[]{:S(2)}, u32[]{:S(2)}) %all-to-all-start.5) | async-done | bytes 16416 | tf_op jit(solution)/shard_map/all_to_all | solution.py:79
  21.3 3.5 %all-to-all-start = ((bf16[128,8,256]{0,2,1:T(8,128)(2,1)}), bf16[128,8,256]{0,2,1:T(8,128)(2,1)S(1)}, u32[]{:S(2)}, u32[]{:S(2)}) async-start(bf16[128,8,256]{0,2,1:T(8,128)(2,1)} %bitcast.16), calls=%async_computation | async-start | bytes 1048576 | tf_op jit(solution)/shard_map/all_to_all | solution.py:82
  27.0 8.3 %all-to-all-done = bf16[128,8,256]{0,2,1:T(8,128)(2,1)S(1)} async-done(((bf16[128,8,256]{0,2,1:T(8,128)(2,1)}), bf16[128,8,256]{0,2,1:T(8,128)(2,1)S(1)}, u32[]{:S(2)}, u32[]{:S(2)}) %all-to-all-start) | async-done | bytes 524320 | tf_op jit(solution)/shard_map/all_to_all | solution.py:82
  35.3 6.5 %all-to-all-start.3 = ((bf16[128,8,256]{0,2,1:T(8,128)(2,1)}), bf16[128,8,256]{0,2,1:T(8,128)(2,1)S(1)}, u32[]{:S(2)}, u32[]{:S(2)}) async-start(bf16[128,8,256]{0,2,1:T(8,128)(2,1)} %bitcast.22), calls=%async_computation.3 | async-start | bytes 1048576 | tf_op jit(solution)/shard_map/all_to_all | solution.py:83
  43.2 11.9 %all-to-all-done.3 = bf16[128,8,256]{0,2,1:T(8,128)(2,1)S(1)} async-done(((bf16[128,8,256]{0,2,1:T(8,128)(2,1)}), bf16[128,8,256]{0,2,1:T(8,128)(2,1)S(1)}, u32[]{:S(2)}, u32[]{:S(2)}) %all-to-all-start.3) | async-done | bytes 524320 | tf_op jit(solution)/shard_map/all_to_all | solution.py:83
  55.9 4.2 %all-to-all-start.1 = ((bf16[128,8,512]{0,2,1:T(8,128)(2,1)}), bf16[128,8,512]{0,2,1:T(8,128)(2,1)S(1)}, u32[]{:S(2)}, u32[]{:S(2)}) async-start(bf16[128,8,512]{0,2,1:T(8,128)(2,1)} %bitcast.18), calls=%async_computation.1 | async-start | bytes 2097152 | tf_op jit(solution)/shard_map/all_to_all | solution.py:74
  61.4 23.0 %all-to-all-done.1 = bf16[128,8,512]{0,2,1:T(8,128)(2,1)S(1)} async-done(((bf16[128,8,512]{0,2,1:T(8,128)(2,1)}), bf16[128,8,512]{0,2,1:T(8,128)(2,1)S(1)}, u32[]{:S(2)}, u32[]{:S(2)}) %all-to-all-start.1) | async-done | bytes 1048608 | tf_op jit(solution)/shard_map/all_to_all | solution.py:74
  84.4 5.3 %all-to-all-start.4 = ((bf16[128,8,512]{0,2,1:T(8,128)(2,1)}), bf16[128,8,512]{0,2,1:T(8,128)(2,1)S(1)}, u32[]{:S(2)}, u32[]{:S(2)}) async-start(bf16[128,8,512]{0,2,1:T(8,128)(2,1)} %bitcast.24), calls=%async_computation.4 | async-start | bytes 2097152 | tf_op jit(solution)/shard_map/all_to_all | solution.py:75
  92.1 4.0 %collective-permute-start.1 = (bf16[1024,2,128]{0,2,1:T(8,128)(2,1)}, bf16[1024,2,128]{0,2,1:T(8,128)(2,1)}, u32[]{:S(2)}, u32[]{:S(2)}) collective-permute-start(bf16[1024,2,128]{0,2,1:T(8,128)(2,1)} %reshape.218), channel_id=1, source_target_pairs={{0,8},{8,16},{16,24},{1,9},{9,17},{17,25},{2,10},{10,18},{18,26},{... | collective-permute-start | bytes 1572872 | tf_op jit(solution)/shard_map/ppermute | solution.py:22
  119.6 48.6 %while.21 = (s32[]{:T(128)}, bf16[1024,2,2,128]{0,3,2,1:T(8,128)(2,1)}, f32[2048,2,128]{0,2,1:T(8,128)S(1)}, f32[2048,2,128]{0,2,1:T(8,128)}, bf16[2048,2,128]{0...) while((s32[]{:T(128)}, ...), condition=%wide.region_4.5_spmd, body=%wide.region_3.4_spmd.sunk | while | flops 4062578176 | bytes 158969360 | solution.py:153
  124.5 4.5 %copy-done = f32[2,1536,512,2]{2,1,3,0:T(8,128)} copy-done((f32[2,1536,512,2]{2,1,3,0:T(8,128)}, f32[2,1536,512,2]{2,1,3,0:T(8,128)S(1)}, u32[]{:S(2)}) %copy-start) | copy-done | bytes 12582936 | tf_op jit(solution)/shard_map/while
  132.3 8.1 %fusion.69 = bf16[2,2,512,1536]{2,3,1,0:T(8,128)(2,1)S(1)} fusion(f32[2,1536,512,2]{2,1,3,0:T(8,128)} %copy-done, f32[2,2,512]{2,1,0:T(2,128)S(1)} %get-tuple-element.474, f32[2,2,512]{2,1,0:T(2,128)S(1)} %get-tuple-element.475, pred[512,1536]{0,1:T(8,128)(4,1)S(1)} %and_and_fusion.2, bf16[2048,2,128]{0,2,1:T(8,128)(2,1)S(1)} %copy-done.13, ...), kind=kOutput, calls=%fused_computation.2.clone.1 | convolution fusion | flops 824180736 | bytes 20987912 | tf_op jit(solution)/shard_map/while/body/eval_jaxpr/qgrd,kgd->grqk/dot_general | solution.py:32
  148.9 4.5 %copy-done = f32[2,1536,512,2]{2,1,3,0:T(8,128)} copy-done((f32[2,1536,512,2]{2,1,3,0:T(8,128)}, f32[2,1536,512,2]{2,1,3,0:T(8,128)S(1)}, u32[]{:S(2)}) %copy-start) | copy-done | bytes 12582936 | tf_op jit(solution)/shard_map/while
  156.6 8.1 %fusion.69 = bf16[2,2,512,1536]{2,3,1,0:T(8,128)(2,1)S(1)} fusion(f32[2,1536,512,2]{2,1,3,0:T(8,128)} %copy-done, f32[2,2,512]{2,1,0:T(2,128)S(1)} %get-tuple-element.474, f32[2,2,512]{2,1,0:T(2,128)S(1)} %get-tuple-element.475, pred[512,1536]{0,1:T(8,128)(4,1)S(1)} %and_and_fusion.2, bf16[2048,2,128]{0,2,1:T(8,128)(2,1)S(1)} %copy-done.13, ...), kind=kOutput, calls=%fused_computation.2.clone.1 | convolution fusion | flops 824180736 | bytes 20987912 | tf_op jit(solution)/shard_map/while/body/eval_jaxpr/qgrd,kgd->grqk/dot_general | solution.py:32
  168.3 3.8 %collective-permute-start.2 = (bf16[1024,2,128]{0,2,1:T(8,128)(2,1)S(1)}, bf16[1024,2,128]{0,2,1:T(8,128)(2,1)S(1)}, u32[]{:S(2)}, u32[]{:S(2)}) collective-permute-start(bf16[1024,2,128]{0,2,1:T(8,128)(2,1)S(1)} %slice.67), channel_id=1, source_target_pairs={{8,0},{16,8},{24,16},{9,1},{17,9},{25,17},{10,2},{18,10},{26,18},{... | collective-permute-start | bytes 1572872 | tf_op jit(solution)/shard_map/ppermute | solution.py:22
  172.2 7.8 %collective-permute-done.2 = bf16[1024,2,128]{0,2,1:T(8,128)(2,1)S(1)} collective-permute-done((bf16[1024,2,128]{0,2,1:T(8,128)(2,1)S(1)}, bf16[1024,2,128]{0,2,1:T(8,128)(2,1)S(1)}, u32[]{:S(2)}, u32[]{:S(2)}) %collective-permute-start.2) | collective-permute-done | bytes 524320 | tf_op jit(solution)/shard_map/ppermute | solution.py:22
  181.3 3.9 %all-to-all-start.7 = ((bf16[8,128,256]{2,1,0:T(8,128)(2,1)}), bf16[8,128,256]{2,1,0:T(8,128)(2,1)S(1)}, u32[]{:S(2)}, u32[]{:S(2)}) async-start(bf16[8,128,256]{2,1,0:T(8,128)(2,1)} %copy.153), calls=%async_computation.7 | async-start | bytes 1048576 | tf_op jit(solution)/shard_map/all_to_all | solution.py:176
  188.6 8.6 %collective-permute-done.3 = bf16[1024,2,128]{0,2,1:T(8,128)(2,1)S(1)} collective-permute-done((bf16[1024,2,128]{0,2,1:T(8,128)(2,1)S(1)}, bf16[1024,2,128]{0,2,1:T(8,128)(2,1)S(1)}, u32[]{:S(2)}, u32[]{:S(2)}) %collective-permute-start.3) | collective-permute-done | bytes 524320 | tf_op jit(solution)/shard_map/ppermute | solution.py:22
  199.7 5.4 %all-to-all-start.8 = ((bf16[8,128,256]{2,1,0:T(8,128)(2,1)}), bf16[8,128,256]{2,1,0:T(8,128)(2,1)S(1)}, u32[]{:S(2)}, u32[]{:S(2)}) async-start(bf16[8,128,256]{2,1,0:T(8,128)(2,1)} %copy.154), calls=%async_computation.8 | async-start | bytes 1048576 | tf_op jit(solution)/shard_map/all_to_all | solution.py:179
  206.9 7.4 %all-to-all-done.8 = bf16[8,128,256]{2,1,0:T(8,128)(2,1)S(1)} async-done(((bf16[8,128,256]{2,1,0:T(8,128)(2,1)}), bf16[8,128,256]{2,1,0:T(8,128)(2,1)S(1)}, u32[]{:S(2)}, u32[]{:S(2)}) %all-to-all-start.8) | async-done | bytes 524320 | tf_op jit(solution)/shard_map/all_to_all | solution.py:179
  214.3 3.6 %all-to-all-start.6 = ((bf16[8,128,512]{2,1,0:T(8,128)(2,1)}), bf16[8,128,512]{2,1,0:T(8,128)(2,1)S(1)}, u32[]{:S(2)}, u32[]{:S(2)}) async-start(bf16[8,128,512]{2,1,0:T(8,128)(2,1)} %copy.152), calls=%async_computation.6 | async-start | bytes 2097152 | tf_op jit(solution)/shard_map/all_to_all | solution.py:161
  220.5 19.2 %all-to-all-done.6 = bf16[8,128,512]{2,1,0:T(8,128)(2,1)S(1)} async-done(((bf16[8,128,512]{2,1,0:T(8,128)(2,1)}), bf16[8,128,512]{2,1,0:T(8,128)(2,1)S(1)}, u32[]{:S(2)}, u32[]{:S(2)}) %all-to-all-start.6) | async-done | bytes 1048608 | tf_op jit(solution)/shard_map/all_to_all | solution.py:161
  (119 shorter events, 75.5 us)
Async XLA Ops:
  0.6 11.8 %all-to-all-start.2 = ((f32[128,8,4]{0,2,1:T(4,128)}), f32[128,8,4]{0,2,1:T(4,128)S(1)}, u32[]{:S(2)}, u32[]{:S(2)}) async-start(f32[128,8,4]{0,2,1:T(4,128)} %bitcast.171), calls=%async_computation.2 | async-start | bytes 32768 | tf_op jit(solution)/shard_map/all_to_all | solution.py:78
  9.2 32.7 %copy-start.12 = (bf16[128,4096]{1,0:T(8,128)(2,1)S(1)}, bf16[128,4096]{1,0:T(8,128)(2,1)}, u32[]{:S(2)}) copy-start(bf16[128,4096]{1,0:T(8,128)(2,1)} %param.17) | copy-start | bytes 3145732
  12.4 8.9 %all-to-all-start.5 = ((f32[128,8,4]{0,2,1:T(4,128)}), f32[128,8,4]{0,2,1:T(4,128)S(1)}, u32[]{:S(2)}, u32[]{:S(2)}) async-start(f32[128,8,4]{0,2,1:T(4,128)} %bitcast.26), calls=%async_computation.5 | async-start | bytes 32768 | tf_op jit(solution)/shard_map/all_to_all | solution.py:79
  21.3 14.0 %all-to-all-start = ((bf16[128,8,256]{0,2,1:T(8,128)(2,1)}), bf16[128,8,256]{0,2,1:T(8,128)(2,1)S(1)}, u32[]{:S(2)}, u32[]{:S(2)}) async-start(bf16[128,8,256]{0,2,1:T(8,128)(2,1)} %bitcast.16), calls=%async_computation | async-start | bytes 1048576 | tf_op jit(solution)/shard_map/all_to_all | solution.py:82
  24.8 35.2 %copy-start.7 = (bf16[128,4096]{1,0:T(8,128)(2,1)S(1)}, bf16[128,4096]{1,0:T(8,128)(2,1)}, u32[]{:S(2)}) copy-start(bf16[128,4096]{1,0:T(8,128)(2,1)} %param.20) | copy-start | bytes 3145732
  35.3 19.8 %copy-start.8 = (bf16[128,8,256]{0,2,1:T(8,128)(2,1)}, bf16[128,8,256]{0,2,1:T(8,128)(2,1)S(1)}, u32[]{:S(2)}) copy-start(bf16[128,8,256]{0,2,1:T(8,128)(2,1)S(1)} %all-to-all-done) | copy-start | bytes 1572868
  35.3 19.8 %all-to-all-start.3 = ((bf16[128,8,256]{0,2,1:T(8,128)(2,1)}), bf16[128,8,256]{0,2,1:T(8,128)(2,1)S(1)}, u32[]{:S(2)}, u32[]{:S(2)}) async-start(bf16[128,8,256]{0,2,1:T(8,128)(2,1)} %bitcast.22), calls=%async_computation.3 | async-start | bytes 1048576 | tf_op jit(solution)/shard_map/all_to_all | solution.py:83
  55.9 28.5 %all-to-all-start.1 = ((bf16[128,8,512]{0,2,1:T(8,128)(2,1)}), bf16[128,8,512]{0,2,1:T(8,128)(2,1)S(1)}, u32[]{:S(2)}, u32[]{:S(2)}) async-start(bf16[128,8,512]{0,2,1:T(8,128)(2,1)} %bitcast.18), calls=%async_computation.1 | async-start | bytes 2097152 | tf_op jit(solution)/shard_map/all_to_all | solution.py:74
  61.4 34.8 %copy-start.9 = (bf16[128,8,256]{0,2,1:T(8,128)(2,1)S(1)}, bf16[128,8,256]{0,2,1:T(8,128)(2,1)}, u32[]{:S(2)}) copy-start(bf16[128,8,256]{0,2,1:T(8,128)(2,1)} %copy-done.8) | copy-start | bytes 1572868
  84.4 14.5 %copy-start.15 = (s32[9]{0:T(128)S(1)}, s32[9]{0:T(128)}, u32[]{:S(2)}) copy-start(s32[9]{0:T(128)} %param.22) | copy-start | bytes 112
  84.4 30.4 %all-to-all-start.4 = ((bf16[128,8,512]{0,2,1:T(8,128)(2,1)}), bf16[128,8,512]{0,2,1:T(8,128)(2,1)S(1)}, u32[]{:S(2)}, u32[]{:S(2)}) async-start(bf16[128,8,512]{0,2,1:T(8,128)(2,1)} %bitcast.24), calls=%async_computation.4 | async-start | bytes 2097152 | tf_op jit(solution)/shard_map/all_to_all | solution.py:75
  92.1 10.4 %collective-permute-start.1 = (bf16[1024,2,128]{0,2,1:T(8,128)(2,1)}, bf16[1024,2,128]{0,2,1:T(8,128)(2,1)}, u32[]{:S(2)}, u32[]{:S(2)}) collective-permute-start(bf16[1024,2,128]{0,2,1:T(8,128)(2,1)} %reshape.218), channel_id=1, source_target_pairs={{0,8},{8,16},{16,24},{1,9},{9,17},{17,25},{2,10},{10,18},{18,26},{... | collective-permute-start | bytes 1572872 | tf_op jit(solution)/shard_map/ppermute | solution.py:22
  96.7 8.1 %copy-start.11 = (bf16[1024,2,128]{0,2,1:T(8,128)(2,1)}, bf16[1024,2,128]{0,2,1:T(8,128)(2,1)S(1)}, u32[]{:S(2)}) copy-start(bf16[1024,2,128]{0,2,1:T(8,128)(2,1)S(1)} %reshape.215) | copy-start | bytes 1572868
  96.8 11.3 %collective-permute-start = (bf16[1024,2,128]{0,2,1:T(8,128)(2,1)S(1)}, bf16[1024,2,128]{0,2,1:T(8,128)(2,1)}, u32[]{:S(2)}, u32[]{:S(2)}) collective-permute-start(bf16[1024,2,128]{0,2,1:T(8,128)(2,1)S(1)} %reshape.215), channel_id=1, source_target_pairs={{0,8},{8,16},{16,24},{1,9},{9,17},{17,25},{2,10},{10,18},{18,26},{... | collective-permute-start | bytes 1572872 | tf_op jit(solution)/shard_map/ppermute | solution.py:22
  132.2 8.1 %copy-start.3 = (f32[2048,2,128]{0,2,1:T(8,128)}, f32[2048,2,128]{0,2,1:T(8,128)S(1)}, u32[]{:S(2)}) copy-start(f32[2048,2,128]{0,2,1:T(8,128)S(1)} %fusion.72) | copy-start | bytes 6291460 | tf_op jit(solution)/shard_map/while
  132.3 8.1 %copy-start.4 = (bf16[1024,2,2,128]{0,3,2,1:T(8,128)(2,1)S(1)}, bf16[1024,2,2,128]{0,3,2,1:T(8,128)(2,1)}, u32[]{:S(2)}) copy-start(bf16[1024,2,2,128]{0,3,2,1:T(8,128)(2,1)} %get-tuple-element.498) | copy-start | bytes 3145732 | tf_op jit(solution)/shard_map/while
  156.6 8.1 %copy-start.3 = (f32[2048,2,128]{0,2,1:T(8,128)}, f32[2048,2,128]{0,2,1:T(8,128)S(1)}, u32[]{:S(2)}) copy-start(f32[2048,2,128]{0,2,1:T(8,128)S(1)} %fusion.72) | copy-start | bytes 6291460 | tf_op jit(solution)/shard_map/while
  156.6 8.1 %copy-start.4 = (bf16[1024,2,2,128]{0,3,2,1:T(8,128)(2,1)S(1)}, bf16[1024,2,2,128]{0,3,2,1:T(8,128)(2,1)}, u32[]{:S(2)}) copy-start(bf16[1024,2,2,128]{0,3,2,1:T(8,128)(2,1)} %get-tuple-element.498) | copy-start | bytes 3145732 | tf_op jit(solution)/shard_map/while
  168.3 11.6 %collective-permute-start.2 = (bf16[1024,2,128]{0,2,1:T(8,128)(2,1)S(1)}, bf16[1024,2,128]{0,2,1:T(8,128)(2,1)S(1)}, u32[]{:S(2)}, u32[]{:S(2)}) collective-permute-start(bf16[1024,2,128]{0,2,1:T(8,128)(2,1)S(1)} %slice.67), channel_id=1, source_target_pairs={{8,0},{16,8},{24,16},{9,1},{17,9},{25,17},{10,2},{18,10},{26,18},{... | collective-permute-start | bytes 1572872 | tf_op jit(solution)/shard_map/ppermute | solution.py:22
  181.3 18.4 %all-to-all-start.7 = ((bf16[8,128,256]{2,1,0:T(8,128)(2,1)}), bf16[8,128,256]{2,1,0:T(8,128)(2,1)S(1)}, u32[]{:S(2)}, u32[]{:S(2)}) async-start(bf16[8,128,256]{2,1,0:T(8,128)(2,1)} %copy.153), calls=%async_computation.7 | async-start | bytes 1048576 | tf_op jit(solution)/shard_map/all_to_all | solution.py:176
  185.2 19.9 %copy-start.6 = (bf16[1024,2,2,128]{0,3,2,1:T(8,128)(2,1)S(1)}, bf16[1024,2,2,128]{0,3,2,1:T(8,128)(2,1)}, u32[]{:S(2)}) copy-start(bf16[1024,2,2,128]{0,3,2,1:T(8,128)(2,1)} %get-tuple-element.274) | copy-start | bytes 3145732
  186.6 10.5 %collective-permute-start.3 = (bf16[1024,2,128]{0,2,1:T(8,128)(2,1)S(1)}, bf16[1024,2,128]{0,2,1:T(8,128)(2,1)S(1)}, u32[]{:S(2)}, u32[]{:S(2)}) collective-permute-start(bf16[1024,2,128]{0,2,1:T(8,128)(2,1)S(1)} %slice.66), channel_id=1, source_target_pairs={{8,0},{16,8},{24,16},{9,1},{17,9},{25,17},{10,2},{18,10},{26,18},{... | collective-permute-start | bytes 1572872 | tf_op jit(solution)/shard_map/ppermute | solution.py:22
  199.7 14.6 %all-to-all-start.8 = ((bf16[8,128,256]{2,1,0:T(8,128)(2,1)}), bf16[8,128,256]{2,1,0:T(8,128)(2,1)S(1)}, u32[]{:S(2)}, u32[]{:S(2)}) async-start(bf16[8,128,256]{2,1,0:T(8,128)(2,1)} %copy.154), calls=%async_computation.8 | async-start | bytes 1048576 | tf_op jit(solution)/shard_map/all_to_all | solution.py:179
  214.3 25.4 %all-to-all-start.6 = ((bf16[8,128,512]{2,1,0:T(8,128)(2,1)}), bf16[8,128,512]{2,1,0:T(8,128)(2,1)S(1)}, u32[]{:S(2)}, u32[]{:S(2)}) async-start(bf16[8,128,512]{2,1,0:T(8,128)(2,1)} %copy.152), calls=%async_computation.6 | async-start | bytes 2097152 | tf_op jit(solution)/shard_map/all_to_all | solution.py:161
  (13 other events, 53.6 us)
where the time goes:
time: 243 us; the launch traced here: 242 us
  waiting for transfers between devices  99.6 us (41%)
  starting transfers between devices  54.1 us (22%)
  local copies, waits for them, and re-layouts  40.6 us (17%)
  matrix products  35.3 us (15%)
  other arithmetic  10.8 us (4%)
    all_to_all x1, waiting for transfers between devices, shards(): lax.all_to_all(query, 'head', split_axis=1, concat_axis=0, tiled=True)  23 us
    ppermute x4, waiting for transfers between devices, from_behind(): lax.ppermute(value, axis, [(source, source + steps) for source in range(l...  22.9 us
    all_to_all x1, waiting for transfers between devices, shards(): lax.all_to_all(query_low, 'head', split_axis=0, concat_axis=1, tiled=True)  19.2 us
    dot_general x2, matrix products, tile_grads(): jnp.einsum('qgrd,kgd->grqk', grad_rows, value_window, preferred_element_t...  16.2 us
    all_to_all x1, waiting for transfers between devices, shards(): lax.all_to_all(value_matrix, 'head', split_axis=1, concat_axis=0, tiled=T...  11.9 us
    ppermute x4, starting transfers between devices, from_behind(): lax.ppermute(value, axis, [(source, source + steps) for source in range(l...  11.8 us
    unnamed x27, local copies, waits for them, and re-layouts  11.8 us
    while x32, local copies, waits for them, and re-layouts  9.4 us
  transfers between devices with their start and end apart: 13, of which 12 were waited for; matrix products, arithmetic and copies ran while one was open for 12% of the time, Pallas kernels for 0%

commit v1 on v0

--- a/solution.py
+++ b/solution.py
@@ -8,6 +8,13 @@
 DOCHALF = 512
 QBLK = 512
 attn_scale = 144.0 ** (-0.5)
+
+
+def stacked_exchange(x, axis, split, join):
+    size = lax.axis_size(axis)
+    blocks = jnp.stack(jnp.split(x, size, axis=split), axis=0)
+    blocks = lax.all_to_all(blocks, axis, split_axis=0, concat_axis=0)
+    return jnp.concatenate(blocks, axis=join)
 
 
 def partner(value, axis, apart):
@@ -71,7 +78,7 @@
         axis=2,
     )
     query_heads, grad_heads = (
-        lax.all_to_all(query, "head", split_axis=1, concat_axis=0, tiled=True),
+        stacked_exchange(query, "head", 1, 0),
         lax.all_to_all(output_gradient, "head", split_axis=1, concat_axis=0, tiled=True),
     )
     lse_heads, delta_heads = (

time: 243 us -> 242 us (level)
  local copies, waits for them, and re-layouts: 40.6 us -> 49.1 us
  waiting for transfers between devices: 99.6 us -> 91.8 us
    all_to_all x1, waiting for transfers between devices: 23 us -> 0.63 us  [stacked_exchange(): blocks = lax.all_to_all(blocks, axis, split_axis=0, concat_axis=0)]
    all_to_all x1, waiting for transfers between devices: 1.49 us -> 16 us  [shards(): lax.all_to_all(output_gradient, 'head', split_axis=1, concat_axis=0, tile...]
    unnamed x27, local copies, waits for them, and re-layouts: 11.8 us -> 17 us
    dynamic_slice x0 -> x2, local copies, waits for them, and re-layouts: none -> 2.81 us  [block_step(): query_rows = lax.dynamic_slice_in_dim(query_heads, start, QBLK, 0)]
    while x32 -> x28, local copies, waits for them, and re-layouts: 9.4 us -> 9.08 us
  transfers between devices with their start and end apart: 13 -> 13, of which waited for: 12 -> 12; matrix products, arithmetic and copies ran while one was open for 12% -> 15% of each run, Pallas kernels for 0% -> 0%
where the time goes in v1:
time: 242 us; the launch traced here: 241 us
  waiting for transfers between devices  91.8 us (38%)
  starting transfers between devices  54.9 us (23%)
  local copies, waits for them, and re-layouts  49.1 us (20%)
  matrix products  33.1 us (14%)
  other arithmetic  10.9 us (5%)
    ppermute x4, waiting for transfers between devices, from_behind(): lax.ppermute(value, axis, [(source, source + steps) for source in range(l...  22.9 us
    all_to_all x1, waiting for transfers between devices, shards(): lax.all_to_all(query_low, 'head', split_axis=0, concat_axis=1, tiled=True)  19.2 us
    unnamed x27, local copies, waits for them, and re-layouts  17 us
    dot_general x2, matrix products, tile_grads(): jnp.einsum('qgrd,kgd->grqk', grad_rows, value_window, preferred_element_t...  16.2 us
    all_to_all x1, waiting for transfers between devices, shards(): lax.all_to_all(output_gradient, 'head', split_axis=1, concat_axis=0, tile...  16 us
    all_to_all x1, waiting for transfers between devices, shards(): lax.all_to_all(value_matrix, 'head', split_axis=1, concat_axis=0, tiled=T...  11.9 us
    ppermute x4, starting transfers between devices, from_behind(): lax.ppermute(value, axis, [(source, source + steps) for source in range(l...  11.9 us
    while x28, local copies, waits for them, and re-layouts  9.08 us
  transfers between devices with their start and end apart: 13, of which 12 were waited for; matrix products, arithmetic and copies ran while one was open for 15% of the time, Pallas kernels for 0%

profile of v1, /device:TPU:1, one launch (start us, length us, event | category | flops | bytes accessed | tf_op | source)
XLA Modules:
  0.0 241.0 jit_solution(16314894781380992240)
XLA Ops:
  0.6 6.4 %all-to-all-start.2 = ((f32[128,8,4]{0,2,1:T(4,128)}), f32[128,8,4]{0,2,1:T(4,128)S(1)}, u32[]{:S(2)}, u32[]{:S(2)}) async-start(f32[128,8,4]{0,2,1:T(4,128)} %bitcast.182), calls=%async_computation.2 | async-start | bytes 32768 | tf_op jit(solution)/shard_map/all_to_all | solution.py:85
  12.4 3.5 %all-to-all-start.5 = ((f32[128,8,4]{0,2,1:T(4,128)}), f32[128,8,4]{0,2,1:T(4,128)S(1)}, u32[]{:S(2)}, u32[]{:S(2)}) async-start(f32[128,8,4]{0,2,1:T(4,128)} %bitcast.32), calls=%async_computation.5 | async-start | bytes 32768 | tf_op jit(solution)/shard_map/all_to_all | solution.py:86
  18.0 3.4 %all-to-all-done.5 = f32[128,8,4]{0,2,1:T(4,128)S(1)} async-done(((f32[128,8,4]{0,2,1:T(4,128)}), f32[128,8,4]{0,2,1:T(4,128)S(1)}, u32[]{:S(2)}, u32[]{:S(2)}) %all-to-all-start.5) | async-done | bytes 16416 | tf_op jit(solution)/shard_map/all_to_all | solution.py:86
  21.3 3.5 %all-to-all-start = ((bf16[128,8,256]{0,2,1:T(8,128)(2,1)}), bf16[128,8,256]{0,2,1:T(8,128)(2,1)S(1)}, u32[]{:S(2)}, u32[]{:S(2)}) async-start(bf16[128,8,256]{0,2,1:T(8,128)(2,1)} %bitcast.16), calls=%async_computation | async-start | bytes 1048576 | tf_op jit(solution)/shard_map/all_to_all | solution.py:89
  26.9 8.4 %all-to-all-done = bf16[128,8,256]{0,2,1:T(8,128)(2,1)S(1)} async-done(((bf16[128,8,256]{0,2,1:T(8,128)(2,1)}), bf16[128,8,256]{0,2,1:T(8,128)(2,1)S(1)}, u32[]{:S(2)}, u32[]{:S(2)}) %all-to-all-start) | async-done | bytes 524320 | tf_op jit(solution)/shard_map/all_to_all | solution.py:89
  35.3 6.5 %all-to-all-start.3 = ((bf16[128,8,256]{0,2,1:T(8,128)(2,1)}), bf16[128,8,256]{0,2,1:T(8,128)(2,1)S(1)}, u32[]{:S(2)}, u32[]{:S(2)}) async-start(bf16[128,8,256]{0,2,1:T(8,128)(2,1)} %bitcast.28), calls=%async_computation.3 | async-start | bytes 1048576 | tf_op jit(solution)/shard_map/all_to_all | solution.py:90
  43.2 11.9 %all-to-all-done.3 = bf16[128,8,256]{0,2,1:T(8,128)(2,1)S(1)} async-done(((bf16[128,8,256]{0,2,1:T(8,128)(2,1)}), bf16[128,8,256]{0,2,1:T(8,128)(2,1)S(1)}, u32[]{:S(2)}, u32[]{:S(2)}) %all-to-all-start.3) | async-done | bytes 524320 | tf_op jit(solution)/shard_map/all_to_all | solution.py:90
  55.1 4.2 %all-to-all-start.4 = ((bf16[128,8,512]{0,2,1:T(8,128)(2,1)}), bf16[128,8,512]{0,2,1:T(8,128)(2,1)S(1)}, u32[]{:S(2)}, u32[]{:S(2)}) async-start(bf16[128,8,512]{0,2,1:T(8,128)(2,1)} %bitcast.30), calls=%async_computation.4 | async-start | bytes 2097152 | tf_op jit(solution)/shard_map/all_to_all | solution.py:82
  67.6 16.0 %all-to-all-done.4 = bf16[128,8,512]{0,2,1:T(8,128)(2,1)S(1)} async-done(((bf16[128,8,512]{0,2,1:T(8,128)(2,1)}), bf16[128,8,512]{0,2,1:T(8,128)(2,1)S(1)}, u32[]{:S(2)}, u32[]{:S(2)}) %all-to-all-start.4) | async-done | bytes 1048608 | tf_op jit(solution)/shard_map/all_to_all | solution.py:82
  83.6 5.2 %all-to-all-start.1 = ((bf16[8,128,512]{2,1,0:T(8,128)(2,1)}), bf16[8,128,512]{2,1,0:T(8,128)(2,1)S(1)}, u32[]{:S(2)}, u32[]{:S(2)}) async-start(bf16[8,128,512]{2,1,0:T(8,128)(2,1)} %copy-done.8), calls=%async_computation.1 | async-start | bytes 2097152 | tf_op jit(solution)/shard_map/all_to_all | solution.py:16
  92.0 4.0 %collective-permute-start.1 = (bf16[1024,2,128]{0,2,1:T(8,128)(2,1)}, bf16[1024,2,128]{0,2,1:T(8,128)(2,1)}, u32[]{:S(2)}, u32[]{:S(2)}) collective-permute-start(bf16[1024,2,128]{0,2,1:T(8,128)(2,1)} %reshape.210), channel_id=1, source_target_pairs={{0,8},{8,16},{16,24},{1,9},{9,17},{17,25},{2,10},{10,18},{18,26},{... | collective-permute-start | bytes 1572872 | tf_op jit(solution)/shard_map/ppermute | solution.py:29
  117.8 48.9 %while.21 = (s32[]{:T(128)}, bf16[1024,2,2,128]{0,3,2,1:T(8,128)(2,1)}, f32[2048,2,128]{0,2,1:T(8,128)S(1)}, f32[2048,2,128]{0,2,1:T(8,128)}, bf16[2048,2,128]{0...) while((s32[]{:T(128)}, ...), condition=%wide.region_4.5_spmd, body=%wide.region_3.4_spmd.sunk | while | flops 4062578176 | bytes 155823600 | solution.py:160
  123.0 4.5 %copy-done = f32[2,1536,512,2]{2,1,3,0:T(8,128)} copy-done((f32[2,1536,512,2]{2,1,3,0:T(8,128)}, f32[2,1536,512,2]{2,1,3,0:T(8,128)S(1)}, u32[]{:S(2)}) %copy-start) | copy-done | bytes 12582936 | tf_op jit(solution)/shard_map/while
  130.7 8.1 %fusion.68 = bf16[2,2,512,1536]{2,3,1,0:T(8,128)(2,1)S(1)} fusion(f32[2,1536,512,2]{2,1,3,0:T(8,128)} %copy-done, f32[2,2,512]{2,1,0:T(2,128)S(1)} %get-tuple-element.474, f32[2,2,512]{2,1,0:T(2,128)S(1)} %get-tuple-element.475, pred[512,1536]{0,1:T(8,128)(4,1)S(1)} %and_and_fusion.2, bf16[2048,2,128]{0,2,1:T(8,128)(2,1)S(1)} %copy-done.9, ...), kind=kOutput, calls=%fused_computation.2.clone.1 | convolution fusion | flops 824180736 | bytes 20987912 | tf_op jit(solution)/shard_map/while/body/eval_jaxpr/qgrd,kgd->grqk/dot_general | solution.py:39
  147.5 4.5 %copy-done = f32[2,1536,512,2]{2,1,3,0:T(8,128)} copy-done((f32[2,1536,512,2]{2,1,3,0:T(8,128)}, f32[2,1536,512,2]{2,1,3,0:T(8,128)S(1)}, u32[]{:S(2)}) %copy-start) | copy-done | bytes 12582936 | tf_op jit(solution)/shard_map/while
  155.2 8.1 %fusion.68 = bf16[2,2,512,1536]{2,3,1,0:T(8,128)(2,1)S(1)} fusion(f32[2,1536,512,2]{2,1,3,0:T(8,128)} %copy-done, f32[2,2,512]{2,1,0:T(2,128)S(1)} %get-tuple-element.474, f32[2,2,512]{2,1,0:T(2,128)S(1)} %get-tuple-element.475, pred[512,1536]{0,1:T(8,128)(4,1)S(1)} %and_and_fusion.2, bf16[2048,2,128]{0,2,1:T(8,128)(2,1)S(1)} %copy-done.9, ...), kind=kOutput, calls=%fused_computation.2.clone.1 | convolution fusion | flops 824180736 | bytes 20987912 | tf_op jit(solution)/shard_map/while/body/eval_jaxpr/qgrd,kgd->grqk/dot_general | solution.py:39
  166.9 3.8 %collective-permute-start.2 = (bf16[1024,2,128]{0,2,1:T(8,128)(2,1)S(1)}, bf16[1024,2,128]{0,2,1:T(8,128)(2,1)S(1)}, u32[]{:S(2)}, u32[]{:S(2)}) collective-permute-start(bf16[1024,2,128]{0,2,1:T(8,128)(2,1)S(1)} %slice.67), channel_id=1, source_target_pairs={{8,0},{16,8},{24,16},{9,1},{17,9},{25,17},{10,2},{18,10},{26,18},{... | collective-permute-start | bytes 1572872 | tf_op jit(solution)/shard_map/ppermute | solution.py:29
  170.7 7.7 %collective-permute-done.2 = bf16[1024,2,128]{0,2,1:T(8,128)(2,1)S(1)} collective-permute-done((bf16[1024,2,128]{0,2,1:T(8,128)(2,1)S(1)}, bf16[1024,2,128]{0,2,1:T(8,128)(2,1)S(1)}, u32[]{:S(2)}, u32[]{:S(2)}) %collective-permute-start.2) | collective-permute-done | bytes 524320 | tf_op jit(solution)/shard_map/ppermute | solution.py:29
  179.8 4.8 %all-to-all-start.7 = ((bf16[8,128,256]{2,1,0:T(8,128)(2,1)}), bf16[8,128,256]{2,1,0:T(8,128)(2,1)S(1)}, u32[]{:S(2)}, u32[]{:S(2)}) async-start(bf16[8,128,256]{2,1,0:T(8,128)(2,1)} %copy.152), calls=%async_computation.7 | async-start | bytes 1048576 | tf_op jit(solution)/shard_map/all_to_all | solution.py:183
  188.0 8.6 %collective-permute-done.3 = bf16[1024,2,128]{0,2,1:T(8,128)(2,1)S(1)} collective-permute-done((bf16[1024,2,128]{0,2,1:T(8,128)(2,1)S(1)}, bf16[1024,2,128]{0,2,1:T(8,128)(2,1)S(1)}, u32[]{:S(2)}, u32[]{:S(2)}) %collective-permute-start.3) | collective-permute-done | bytes 524320 | tf_op jit(solution)/shard_map/ppermute | solution.py:29
  199.1 5.4 %all-to-all-start.8 = ((bf16[8,128,256]{2,1,0:T(8,128)(2,1)}), bf16[8,128,256]{2,1,0:T(8,128)(2,1)S(1)}, u32[]{:S(2)}, u32[]{:S(2)}) async-start(bf16[8,128,256]{2,1,0:T(8,128)(2,1)} %copy.153), calls=%async_computation.8 | async-start | bytes 1048576 | tf_op jit(solution)/shard_map/all_to_all | solution.py:186
  206.3 7.4 %all-to-all-done.8 = bf16[8,128,256]{2,1,0:T(8,128)(2,1)S(1)} async-done(((bf16[8,128,256]{2,1,0:T(8,128)(2,1)}), bf16[8,128,256]{2,1,0:T(8,128)(2,1)S(1)}, u32[]{:S(2)}, u32[]{:S(2)}) %all-to-all-start.8) | async-done | bytes 524320 | tf_op jit(solution)/shard_map/all_to_all | solution.py:186
  213.7 3.6 %all-to-all-start.6 = ((bf16[8,128,512]{2,1,0:T(8,128)(2,1)}), bf16[8,128,512]{2,1,0:T(8,128)(2,1)S(1)}, u32[]{:S(2)}, u32[]{:S(2)}) async-start(bf16[8,128,512]{2,1,0:T(8,128)(2,1)} %copy.151), calls=%async_computation.6 | async-start | bytes 2097152 | tf_op jit(solution)/shard_map/all_to_all | solution.py:168
  219.9 19.2 %all-to-all-done.6 = bf16[8,128,512]{2,1,0:T(8,128)(2,1)S(1)} async-done(((bf16[8,128,512]{2,1,0:T(8,128)(2,1)}), bf16[8,128,512]{2,1,0:T(8,128)(2,1)S(1)}, u32[]{:S(2)}, u32[]{:S(2)}) %all-to-all-start.6) | async-done | bytes 1048608 | tf_op jit(solution)/shard_map/all_to_all | solution.py:168
  (117 shorter events, 81.1 us)
Async XLA Ops:
  0.6 11.8 %all-to-all-start.2 = ((f32[128,8,4]{0,2,1:T(4,128)}), f32[128,8,4]{0,2,1:T(4,128)S(1)}, u32[]{:S(2)}, u32[]{:S(2)}) async-start(f32[128,8,4]{0,2,1:T(4,128)} %bitcast.182), calls=%async_computation.2 | async-start | bytes 32768 | tf_op jit(solution)/shard_map/all_to_all | solution.py:85
  9.2 32.7 %copy-start.6 = (bf16[128,4096]{1,0:T(8,128)(2,1)S(1)}, bf16[128,4096]{1,0:T(8,128)(2,1)}, u32[]{:S(2)}) copy-start(bf16[128,4096]{1,0:T(8,128)(2,1)} %param.20) | copy-start | bytes 3145732
  12.4 8.9 %all-to-all-start.5 = ((f32[128,8,4]{0,2,1:T(4,128)}), f32[128,8,4]{0,2,1:T(4,128)S(1)}, u32[]{:S(2)}, u32[]{:S(2)}) async-start(f32[128,8,4]{0,2,1:T(4,128)} %bitcast.32), calls=%async_computation.5 | async-start | bytes 32768 | tf_op jit(solution)/shard_map/all_to_all | solution.py:86
  21.3 14.0 %all-to-all-start = ((bf16[128,8,256]{0,2,1:T(8,128)(2,1)}), bf16[128,8,256]{0,2,1:T(8,128)(2,1)S(1)}, u32[]{:S(2)}, u32[]{:S(2)}) async-start(bf16[128,8,256]{0,2,1:T(8,128)(2,1)} %bitcast.16), calls=%async_computation | async-start | bytes 1048576 | tf_op jit(solution)/shard_map/all_to_all | solution.py:89
  35.3 19.8 %all-to-all-start.3 = ((bf16[128,8,256]{0,2,1:T(8,128)(2,1)}), bf16[128,8,256]{0,2,1:T(8,128)(2,1)S(1)}, u32[]{:S(2)}, u32[]{:S(2)}) async-start(bf16[128,8,256]{0,2,1:T(8,128)(2,1)} %bitcast.28), calls=%async_computation.3 | async-start | bytes 1048576 | tf_op jit(solution)/shard_map/all_to_all | solution.py:90
  55.1 28.5 %all-to-all-start.4 = ((bf16[128,8,512]{0,2,1:T(8,128)(2,1)}), bf16[128,8,512]{0,2,1:T(8,128)(2,1)S(1)}, u32[]{:S(2)}, u32[]{:S(2)}) async-start(bf16[128,8,512]{0,2,1:T(8,128)(2,1)} %bitcast.30), calls=%async_computation.4 | async-start | bytes 2097152 | tf_op jit(solution)/shard_map/all_to_all | solution.py:82
  67.6 31.1 %copy-start.11 = (s32[9]{0:T(128)S(1)}, s32[9]{0:T(128)}, u32[]{:S(2)}) copy-start(s32[9]{0:T(128)} %param.22) | copy-start | bytes 112
  83.6 30.2 %all-to-all-start.1 = ((bf16[8,128,512]{2,1,0:T(8,128)(2,1)}), bf16[8,128,512]{2,1,0:T(8,128)(2,1)S(1)}, u32[]{:S(2)}, u32[]{:S(2)}) async-start(bf16[8,128,512]{2,1,0:T(8,128)(2,1)} %copy-done.8), calls=%async_computation.1 | async-start | bytes 2097152 | tf_op jit(solution)/shard_map/all_to_all | solution.py:16
  92.0 10.4 %collective-permute-start.1 = (bf16[1024,2,128]{0,2,1:T(8,128)(2,1)}, bf16[1024,2,128]{0,2,1:T(8,128)(2,1)}, u32[]{:S(2)}, u32[]{:S(2)}) collective-permute-start(bf16[1024,2,128]{0,2,1:T(8,128)(2,1)} %reshape.210), channel_id=1, source_target_pairs={{0,8},{8,16},{16,24},{1,9},{9,17},{17,25},{2,10},{10,18},{18,26},{... | collective-permute-start | bytes 1572872 | tf_op jit(solution)/shard_map/ppermute | solution.py:29
  96.6 8.1 %copy-start.7 = (bf16[1024,2,128]{0,2,1:T(8,128)(2,1)}, bf16[1024,2,128]{0,2,1:T(8,128)(2,1)S(1)}, u32[]{:S(2)}) copy-start(bf16[1024,2,128]{0,2,1:T(8,128)(2,1)S(1)} %reshape.208) | copy-start | bytes 1572868
  96.6 11.3 %collective-permute-start = (bf16[1024,2,128]{0,2,1:T(8,128)(2,1)S(1)}, bf16[1024,2,128]{0,2,1:T(8,128)(2,1)}, u32[]{:S(2)}, u32[]{:S(2)}) collective-permute-start(bf16[1024,2,128]{0,2,1:T(8,128)(2,1)S(1)} %reshape.208), channel_id=1, source_target_pairs={{0,8},{8,16},{16,24},{1,9},{9,17},{17,25},{2,10},{10,18},{18,26},{... | collective-permute-start | bytes 1572872 | tf_op jit(solution)/shard_map/ppermute | solution.py:29
  121.1 6.4 %copy-start.1 = (f32[2048,2,128]{0,2,1:T(8,128)S(1)}, f32[2048,2,128]{0,2,1:T(8,128)}, u32[]{:S(2)}) copy-start(f32[2048,2,128]{0,2,1:T(8,128)} %get-tuple-element.500) | copy-start | bytes 6291460 | tf_op jit(solution)/shard_map/while
  121.1 6.4 %copy-start.10 = (bf16[1024,2,2,128]{0,3,2,1:T(8,128)(2,1)S(1)}, bf16[1024,2,2,128]{0,3,2,1:T(8,128)(2,1)}, u32[]{:S(2)}) copy-start(bf16[1024,2,2,128]{0,3,2,1:T(8,128)(2,1)} %get-tuple-element.528) | copy-start | bytes 3145732 | tf_op jit(solution)/shard_map/while
  130.7 8.1 %copy-start.2 = (f32[2048,2,128]{0,2,1:T(8,128)}, f32[2048,2,128]{0,2,1:T(8,128)S(1)}, u32[]{:S(2)}) copy-start(f32[2048,2,128]{0,2,1:T(8,128)S(1)} %fusion.71) | copy-start | bytes 6291460 | tf_op jit(solution)/shard_map/while
  130.7 8.1 %copy-start.3 = (bf16[1024,2,2,128]{0,3,2,1:T(8,128)(2,1)S(1)}, bf16[1024,2,2,128]{0,3,2,1:T(8,128)(2,1)}, u32[]{:S(2)}) copy-start(bf16[1024,2,2,128]{0,3,2,1:T(8,128)(2,1)} %get-tuple-element.498) | copy-start | bytes 3145732 | tf_op jit(solution)/shard_map/while
  145.6 6.4 %copy-start.1 = (f32[2048,2,128]{0,2,1:T(8,128)S(1)}, f32[2048,2,128]{0,2,1:T(8,128)}, u32[]{:S(2)}) copy-start(f32[2048,2,128]{0,2,1:T(8,128)} %get-tuple-element.500) | copy-start | bytes 6291460 | tf_op jit(solution)/shard_map/while
  155.2 8.1 %copy-start.2 = (f32[2048,2,128]{0,2,1:T(8,128)}, f32[2048,2,128]{0,2,1:T(8,128)S(1)}, u32[]{:S(2)}) copy-start(f32[2048,2,128]{0,2,1:T(8,128)S(1)} %fusion.71) | copy-start | bytes 6291460 | tf_op jit(solution)/shard_map/while
  155.2 8.1 %copy-start.3 = (bf16[1024,2,2,128]{0,3,2,1:T(8,128)(2,1)S(1)}, bf16[1024,2,2,128]{0,3,2,1:T(8,128)(2,1)}, u32[]{:S(2)}) copy-start(bf16[1024,2,2,128]{0,3,2,1:T(8,128)(2,1)} %get-tuple-element.498) | copy-start | bytes 3145732 | tf_op jit(solution)/shard_map/while
  166.9 11.6 %collective-permute-start.2 = (bf16[1024,2,128]{0,2,1:T(8,128)(2,1)S(1)}, bf16[1024,2,128]{0,2,1:T(8,128)(2,1)S(1)}, u32[]{:S(2)}, u32[]{:S(2)}) collective-permute-start(bf16[1024,2,128]{0,2,1:T(8,128)(2,1)S(1)} %slice.67), channel_id=1, source_target_pairs={{8,0},{16,8},{24,16},{9,1},{17,9},{25,17},{10,2},{18,10},{26,18},{... | collective-permute-start | bytes 1572872 | tf_op jit(solution)/shard_map/ppermute | solution.py:29
  179.8 19.3 %all-to-all-start.7 = ((bf16[8,128,256]{2,1,0:T(8,128)(2,1)}), bf16[8,128,256]{2,1,0:T(8,128)(2,1)S(1)}, u32[]{:S(2)}, u32[]{:S(2)}) async-start(bf16[8,128,256]{2,1,0:T(8,128)(2,1)} %copy.152), calls=%async_computation.7 | async-start | bytes 1048576 | tf_op jit(solution)/shard_map/all_to_all | solution.py:183
  184.6 19.9 %copy-start.5 = (bf16[1024,2,2,128]{0,3,2,1:T(8,128)(2,1)S(1)}, bf16[1024,2,2,128]{0,3,2,1:T(8,128)(2,1)}, u32[]{:S(2)}) copy-start(bf16[1024,2,2,128]{0,3,2,1:T(8,128)(2,1)} %get-tuple-element.274) | copy-start | bytes 3145732
  186.0 10.5 %collective-permute-start.3 = (bf16[1024,2,128]{0,2,1:T(8,128)(2,1)S(1)}, bf16[1024,2,128]{0,2,1:T(8,128)(2,1)S(1)}, u32[]{:S(2)}, u32[]{:S(2)}) collective-permute-start(bf16[1024,2,128]{0,2,1:T(8,128)(2,1)S(1)} %slice.66), channel_id=1, source_target_pairs={{8,0},{16,8},{24,16},{9,1},{17,9},{25,17},{10,2},{18,10},{26,18},{... | collective-permute-start | bytes 1572872 | tf_op jit(solution)/shard_map/ppermute | solution.py:29
  199.1 14.6 %all-to-all-start.8 = ((bf16[8,128,256]{2,1,0:T(8,128)(2,1)}), bf16[8,128,256]{2,1,0:T(8,128)(2,1)S(1)}, u32[]{:S(2)}, u32[]{:S(2)}) async-start(bf16[8,128,256]{2,1,0:T(8,128)(2,1)} %copy.153), calls=%async_computation.8 | async-start | bytes 1048576 | tf_op jit(solution)/shard_map/all_to_all | solution.py:186
  213.7 25.4 %all-to-all-start.6 = ((bf16[8,128,512]{2,1,0:T(8,128)(2,1)}), bf16[8,128,512]{2,1,0:T(8,128)(2,1)S(1)}, u32[]{:S(2)}, u32[]{:S(2)}) async-start(bf16[8,128,512]{2,1,0:T(8,128)(2,1)} %copy.151), calls=%async_computation.6 | async-start | bytes 2097152 | tf_op jit(solution)/shard_map/all_to_all | solution.py:168
  (8 other events, 27.6 us)
